TPU v7x, 256 devices: a 2x2x32 block of a 4x8x32 slice. The times are simulated.
256 devices in a mesh: ens: 4 (over y, x), region: 32 (over z), feat: 2 (over core).
Axes of the slice: x: 2, y: 2, z: 32, core: 2. Of those that a mesh axis runs over, the one named last changes fastest.
The devices are a block of a 4x8x32 slice.
Arguments:
- grid_lat: bfloat16 [131072, 512], P(('ens', 'region', 'feat')), parts along dimension 0, may hold values from -6 to 6
- g2m_edge: bfloat16 [262144, 512], P(('ens', 'region', 'feat')), parts along dimension 0, may hold values from -6 to 6
- g2m_src: int32 [262144], P(('ens', 'region', 'feat')), parts along dimension 0, may hold values from 0 to 32767, as said below
- g2m_owner: int32 [262144, 1], P(('ens', 'region', 'feat')), parts along dimension 0, may hold values from 0 to 63; in each aligned block of 1024 rows (0 to 1023, 1024 to 2047, ...) at most 32 rows name the same one
- g2m_row: int32 [262144], P(('ens', 'region', 'feat')), parts along dimension 0, may hold values from 0 to 255
- mesh_lat: bfloat16 [65536, 512], P(('ens', 'region', 'feat')), parts along dimension 0, may hold values from -6 to 6
- m2m_edge: bfloat16 [65536, 8, 512], P(('ens', 'region', 'feat')), parts along dimension 0, may hold values from -6 to 6
- m2m_src: int32 [65536, 8], P(('ens', 'region', 'feat')), parts along dimension 0, may hold values from 0 to 16383, as said below
- enc_edge_w: bfloat16 [4, 512, 512], P(None, None, 'feat'), may hold values from -0.25 to 0.25
- enc_node_w: bfloat16 [3, 512, 512], P(None, None, 'feat'), may hold values from -0.25 to 0.25
- proc_edge_w: bfloat16 [2, 4, 512, 512], P(None, None, None, 'feat'), may hold values from -0.25 to 0.25
- proc_node_w: bfloat16 [2, 3, 512, 512], P(None, None, None, 'feat'), may hold values from -0.25 to 0.25
Outputs:
- mesh_out: bfloat16 [65536, 512], P(('ens', 'region', 'feat')), parts along dimension 0
There are 4 independent parts, one for each index of `ens`. A program takes and returns all parts, laid end to end along the dimension named above; an argument that names none is the same for every part. Nothing has to cross between parts.
Inputs may be any that keep to these rules, and one draw needn't show every extreme that they name: Edge i is sent by a grid node of block i // 1024, that is g2m_src[i] // 512 == i // 1024. `g2m_owner`: among the 1024 edges of one block, at most 32 have the same owner. `m2m_src`: for a receiving node v of block b = v // 256, every sender s has s % 256 < 8, or b * 256 - 128 <= s < (b + 1) * 256 + 128.
All inputs are finite; a program needn't handle non-finite values.
Results may differ from a plain program's by a relative error of at most 0.017.
Values may be sent and summed in bfloat16 or wider, within the bound.
No kernel may reach another device: no remote copies, remote signals or barrier semaphores. Data moves between devices by JAX's collectives and lax.ppermute only.
A program may use at most 128 MiB of HBM per device.

v0:
```python
import jax
import jax.numpy as jnp
from jax import lax
from jax.sharding import PartitionSpec as P

MC_DEV = 8


def extended(value, sides, width):
    edges = {}
    for axis, dim in sides:
        size, length = (lax.axis_size(axis), value.shape[dim])
        up = [(i, (i + 1) % size) for i in range(size - 1)]
        last = lax.slice_in_dim(value, length - width, length, axis=dim)
        initial = lax.slice_in_dim(value, 0, width, axis=dim)
        edges[dim] = (
            lax.ppermute(last, axis, up),
            lax.ppermute(initial, axis, [(b, a) for a, b in up]),
        )
    done = []
    for _, dim in sides:
        low, high = edges[dim]
        around = [(width, width) if d in done else (0, 0) for d in range(value.ndim)]
        value = jnp.concatenate([jnp.pad(low, around), value, jnp.pad(high, around)], axis=dim)
        done.append(dim)
    return value


def in_order(pieces, dim):
    dims = list(pieces.shape[1:])
    dims[dim] *= pieces.shape[0]
    return jnp.moveaxis(pieces, 0, dim).reshape(dims)


def all_blocks(value, axes, sequence):
    pieces = value
    for k in sequence:
        pieces = lax.all_gather(pieces, axes[k])
    done = sequence[::-1]
    back = [done.index(k) for k in range(len(axes))]
    pieces = pieces.transpose(*back, *range(len(axes), pieces.ndim))
    return pieces.reshape(-1, *value.shape)


def gather_axes(value, axes, sequence, dim):
    return in_order(all_blocks(value, axes, sequence), dim)


def layer_norm(values):
    center = values - jnp.mean(values, axis=-1, keepdims=True)
    spread = jnp.mean(center * center, axis=-1, keepdims=True)
    return center * lax.rsqrt(spread + 1e-05)


def project(latent, matrix):
    return jnp.dot(latent, matrix, preferred_element_type=jnp.float32).astype(jnp.bfloat16)


def edge_output(pre_act, matrix):
    hidden = jax.nn.silu(pre_act).astype(jnp.bfloat16)
    return layer_norm(jnp.dot(hidden, matrix, preferred_element_type=jnp.float32)).astype(
        jnp.bfloat16
    )


def node_update(latent, aggregate, stack):
    pre_act = jnp.dot(latent, stack[0], preferred_element_type=jnp.float32)
    pre_act = pre_act + jnp.dot(aggregate, stack[1], preferred_element_type=jnp.float32)
    hidden = jax.nn.silu(pre_act).astype(jnp.bfloat16)
    update = layer_norm(jnp.dot(hidden, stack[2], preferred_element_type=jnp.float32))
    return (latent.astype(jnp.float32) + update).astype(jnp.bfloat16)


def widen(stack):
    return lax.all_gather(stack, "feat", axis=2, tiled=True)


def on_device(
    grid_lat,
    g2m_edge,
    g2m_src,
    g2m_owner,
    g2m_row,
    mesh_lat,
    m2m_edge,
    m2m_src,
    enc_edge_w,
    enc_node_w,
    proc_edge_w,
    proc_node_w,
):
    shards = lax.axis_size(("region", "feat"))
    myself = lax.axis_index(("region", "feat"))
    grid_rows = grid_lat.shape[0]
    mesh_rows = mesh_lat.shape[0]
    edge_count = g2m_edge.shape[0]
    width = grid_lat.shape[1]
    capacity = 2 * edge_count // shards
    slot_total = shards * capacity
    edge_stack = widen(enc_edge_w)
    sender = project(grid_lat, edge_stack[1])
    receiver = project(mesh_lat, edge_stack[2])
    local_src = g2m_src - myself * grid_rows
    owner = g2m_owner[:, 0]
    onehot = (owner[:, None] == jnp.arange(shards, dtype=jnp.int32)[None, :]).astype(jnp.int32)
    rank = jnp.sum((jnp.cumsum(onehot, axis=0) - 1) * onehot, axis=1)
    slot = owner * capacity + rank
    slot_edge = (
        jnp.zeros((slot_total,), jnp.int32).at[slot].set(jnp.arange(edge_count, dtype=jnp.int32))
    )
    filled = jnp.zeros((slot_total,), jnp.bool_).at[slot].set(True)
    row_slots = jnp.where(filled, g2m_row[slot_edge], -1).reshape(shards, capacity)
    partial_sum = jnp.dot(g2m_edge, edge_stack[0], preferred_element_type=jnp.float32)
    partial_sum = (partial_sum + sender[local_src].astype(jnp.float32)).astype(jnp.bfloat16)
    packed = partial_sum[slot_edge].reshape(shards, capacity, width)
    got_partial, got_targets = (
        lax.all_to_all(packed, ("region", "feat"), split_axis=0, concat_axis=0, tiled=True),
        lax.all_to_all(row_slots, ("region", "feat"), split_axis=0, concat_axis=0, tiled=True),
    )
    targets = got_targets.reshape(slot_total)
    safe = jnp.maximum(targets, 0)
    pre_act = got_partial.reshape(slot_total, width).astype(jnp.float32) + receiver[safe].astype(
        jnp.float32
    )
    message = edge_output(pre_act, edge_stack[3])
    terms = jnp.where((targets >= 0)[:, None], message.astype(jnp.float32), 0.0)
    aggregate = jax.ops.segment_sum(terms, safe, num_segments=mesh_rows)
    mesh = node_update(mesh_lat, aggregate.astype(jnp.bfloat16), widen(enc_node_w))
    kdeg = m2m_src.shape[1]
    halo_rows = mesh_rows // 2
    senders = m2m_src.reshape(mesh_rows * kdeg)
    home = senders // mesh_rows
    inside = senders % mesh_rows
    table_index = jnp.where(
        inside < MC_DEV,
        mesh_rows + 2 * halo_rows + home * MC_DEV + inside,
        senders - (myself * mesh_rows - halo_rows),
    )
    edges = m2m_edge.reshape(mesh_rows * kdeg, width)
    for layer in range(proc_edge_w.shape[0]):
        layer_edge = widen(proc_edge_w[layer])
        layer_node = widen(proc_node_w[layer])
        sender = project(mesh, layer_edge[1])
        receiver = project(mesh, layer_edge[2])
        bordered = extended(sender, ((("region", "feat"), 0),), halo_rows)
        coarse_rows = gather_axes(sender[:MC_DEV], ("region", "feat"), (0, 1), 0)
        table = jnp.concatenate([bordered, coarse_rows], axis=0)
        pre_act = jnp.dot(edges, layer_edge[0], preferred_element_type=jnp.float32)
        pre_act = (
            pre_act
            + table[table_index].astype(jnp.float32)
            + jnp.repeat(receiver, kdeg, axis=0).astype(jnp.float32)
        )
        message = edge_output(pre_act, layer_edge[3])
        aggregate = jnp.sum(message.astype(jnp.float32).reshape(mesh_rows, kdeg, width), axis=1)
        edges = (edges.astype(jnp.float32) + message.astype(jnp.float32)).astype(jnp.bfloat16)
        mesh = node_update(mesh, aggregate.astype(jnp.bfloat16), layer_node)
    return mesh


def solution(mesh):
    return jax.shard_map(
        on_device,
        mesh=mesh,
        in_specs=(
            P(("ens", "region", "feat"), None),
            P(("ens", "region", "feat"), None),
            P(("ens", "region", "feat")),
            P(("ens", "region", "feat"), None),
            P(("ens", "region", "feat")),
            P(("ens", "region", "feat"), None),
            P(("ens", "region", "feat"), None, None),
            P(("ens", "region", "feat"), None),
            P(None, None, "feat"),
            P(None, None, "feat"),
            P(None, None, None, "feat"),
            P(None, None, None, "feat"),
        ),
        out_specs=P(("ens", "region", "feat"), None),
        check_vma=False,
    )
```

profile of v0, /device:TPU:37, one launch (start us, length us, event | category | flops | bytes accessed | tf_op | source)
XLA Modules:
  0.0 537.7 jit_solution(10828979515456356212)
XLA Ops:
  6.6 0.7 all-gather.17.cloned.1.call-update
  7.3 0.7 fusion.39
  8.0 18.0 %reduce-window.6 = s32[64,8,128]{2,1,0:T(8,128)S(1)} reduce-window(s32[64,8,128]{2,1,0:T(8,128)S(1)} %fusion.39, s32[]{:T(128)} %constant.81.clone.1), window={size=1x1x128 pad=0_0x0_0x127_0}, to_apply=%region_0.0 | reduce-window | flops 8323072 | bytes 524292 | tf_op jit(solution)/shard_map/reduce-window
  26.7 4.3 scatter_custom_fusion.1
  31.1 8.6 %gather_fusion = s32[2048]{0:T(1024)S(1)} fusion(s32[1024]{0:T(1024)S(1)} %copy-done.2, s32[2048]{0:T(1024)S(1)} %fusion.40), kind=kCustom, calls=%fused_computation | custom fusion | bytes 24576 | tf_op jit(solution)/shard_map/gather | solution.py:112
  39.7 4.3 scatter_custom_fusion
  44.0 0.7 all_to_all.9
  44.7 34.3 %all-to-all-start = ((s32[64,1,32]{2,1,0:T(1,128)}), s32[64,1,32]{2,1,0:T(1,128)S(1)}, u32[]{:S(2)}, u32[]{:S(2)}) async-start(s32[64,1,32]{2,1,0:T(1,128)} %bitcast.7), calls=%async_computation | async-start | bytes 65536 | tf_op jit(solution)/shard_map/all_to_all | solution.py:118
  79.1 1.5 convolution_convert_fusion
  80.6 4.0 gather_fusion.1
  84.6 1.7 add_convert_fusion
  86.3 9.2 %gather_fusion.2 = bf16[2048,512]{1,0:T(8,128)(2,1)} fusion(bf16[1024,512]{1,0:T(8,128)(2,1)S(1)} %add_convert_fusion, s32[2048]{0:T(1024)S(1)} %fusion.40), kind=kCustom, calls=%fused_computation.2 | custom fusion | bytes 4202496 | tf_op jit(solution)/shard_map/gather | solution.py:115
  95.5 5.5 %all-to-all-done = s32[64,1,32]{2,1,0:T(1,128)S(1)} async-done(((s32[64,1,32]{2,1,0:T(1,128)}), s32[64,1,32]{2,1,0:T(1,128)S(1)}, u32[]{:S(2)}, u32[]{:S(2)}) %all-to-all-start) | async-done | bytes 8224 | tf_op jit(solution)/shard_map/all_to_all | solution.py:118
  101.0 17.9 %all-to-all-start.1 = ((bf16[64,32,512]{2,1,0:T(8,128)(2,1)}), bf16[64,32,512]{2,1,0:T(8,128)(2,1)}, u32[]{:S(2)}, u32[]{:S(2)}) async-start(bf16[64,32,512]{2,1,0:T(8,128)(2,1)} %bitcast.189), calls=%async_computation.1 | async-start | bytes 4194304 | tf_op jit(solution)/shard_map/all_to_all | solution.py:117
  119.0 0.7 all-gather.15.cloned.1.call-update
  119.8 1.5 fusion.51
  121.4 2.6 fusion.52
  124.1 0.2 all-gather.25.cloned.1.call-start
  124.4 0.4 all-gather.25.cloned.1.call-update
  124.8 0.6 all-gather.23.cloned.1.call-update
  126.1 24.3 %all-gather.15.cloned.1.call-done = bf16[3,512,512]{2,1,0:T(8,128)(2,1)} async-done(((bf16[3,512,256]{2,1,0:T(8,128)(2,1)}), bf16[3,512,512]{2,1,0:T(8,128)(2,1)}) %all-gather.15.cloned.1.call-update) | async-done | bytes 1572880 | tf_op jit(solution)/shard_map/all_gather | solution.py:75
  150.5 2.1 fusion.27
  152.6 1.3 convolution_convert_fusion.5
  154.0 7.5 %gather_fusion.3 = bf16[2048,512]{1,0:T(8,128)(2,1)S(1)} fusion(bf16[256,512]{1,0:T(8,128)(2,1)S(1)} %convolution_convert_fusion.5, s32[2048]{0:T(1024)S(1)} %broadcast_clamp_fusion), kind=kCustom, calls=%fused_computation.3 | custom fusion | bytes 4202496 | tf_op jit(solution)/shard_map/gather | solution.py:122
  161.5 154.8 %all-to-all-done.1 = bf16[64,32,512]{2,1,0:T(8,128)(2,1)} async-done(((bf16[64,32,512]{2,1,0:T(8,128)(2,1)}), bf16[64,32,512]{2,1,0:T(8,128)(2,1)}, u32[]{:S(2)}, u32[]{:S(2)}) %all-to-all-start.1) | async-done | bytes 2097184 | tf_op jit(solution)/shard_map/all_to_all | solution.py:117
  316.4 2.8 multiply_convert_fusion.5
  319.1 2.3 fusion.55
  321.5 0.5 multiply_reduce_fusion.2
  322.0 2.5 convert_select_fusion
  324.5 5.4 %copy.24 = f32[2048,512]{1,0:T(8,128)} copy(f32[2048,512]{0,1:T(8,128)} %convert_select_fusion) | data formatting | bytes 8388608 | tf_op jit(solution)/shard_map/jit(_where)/select_n | solution.py:126
  329.9 14.4 %scatter_custom_fusion.2 = f32[256,512]{1,0:T(8,128)S(1)} fusion(s32[2048]{0:T(1024)S(1)} %reshape.348, f32[2048,512]{1,0:T(8,128)} %copy.24, f32[]{:T(128)} %constant.78.clone.1), kind=kCustom, calls=%fused_computation.96 | custom fusion | flops 1048576 | bytes 524800 | tf_op jit(solution)/shard_map/scatter-add | solution.py:127
  344.3 1.9 fusion.56
  346.2 0.2 multiply_reduce_fusion.5
  346.4 0.2 add_convert_fusion.3
  346.6 1.3 convolution_convert_fusion.4
  348.0 38.9 %all-gather.2 = bf16[256,512]{1,0:T(8,128)(2,1)S(1)} all-gather(bf16[8,512]{1,0:T(8,128)(2,1)S(1)} %slice.172), channel_id=4, replica_groups=mesh['ens'=4,'region'=32,'feat'=2] {'region'}, dimensions={0}, use_global_device_ids=true | all-gather | bytes 270336 | tf_op jit(solution)/shard_map/all_gather | solution.py:38
  386.9 18.3 %all-gather.3 = bf16[64,8,512]{2,1,0:T(8,128)(2,1)S(1)} all-gather(bf16[32,8,512]{2,1,0:T(8,128)(2,1)S(1)} %bitcast.194), channel_id=5, replica_groups=mesh['ens'=4,'region'=32,'feat'=2] {'feat'}, dimensions={0}, use_global_device_ids=true | all-gather | bytes 786432 | tf_op jit(solution)/shard_map/all_gather | solution.py:38
  405.2 3.8 collective-permute-start
  409.0 2.2 collective-permute-start.1
  411.2 1.3 fusion.20
  412.6 1.3 fusion.24
  413.9 1.4 collective-permute-done.1
  415.4 9.2 %gather_fusion.4 = bf16[2048,512]{1,0:T(8,128)(2,1)} fusion(bf16[1024,512]{1,0:T(8,128)(2,1)S(1)} %pad_maximum_fusion, s32[2048]{0:T(1024)S(1)} %broadcast_clamp_fusion.1), kind=kCustom, calls=%fused_computation.4 | custom fusion | bytes 4202496 | tf_op jit(solution)/shard_map/gather | solution.py:151
  424.6 7.2 %fusion.59 = (f32[2048]{0:T(1024)S(1)}, f32[2048,512]{1,0:T(8,128)}) fusion(bf16[1,4,512,512]{3,2,1,0:T(8,128)(2,1)} %all-gather.21.cloned.1.call-done, bf16[2048,512]{1,0:T(8,128)(2,1)} %gather_fusion.4, f32[256,512]{1,0:T(8,128)S(1)} %fusion.20, bf16[256,8,512]{2,1,0:T(8,128)(2,1)} %param.18), kind=kOutput, calls=%fused_computation.143 | convolution fusion | flops 2156918784 | bytes 9969664 | tf_op jit(solution)/shard_map/dot_general | solution.py:61
  431.8 3.0 multiply_reduce_fusion.1
  434.9 0.4 copy-done.3
  435.3 2.7 fusion
  438.0 1.9 fusion.62
  439.9 0.2 multiply_reduce_fusion.4
  440.3 1.3 convolution_convert_fusion.2
  441.6 39.1 %all-gather.6 = bf16[256,512]{1,0:T(8,128)(2,1)S(1)} all-gather(bf16[8,512]{1,0:T(8,128)(2,1)S(1)} %slice.182), channel_id=8, replica_groups=mesh['ens'=4,'region'=32,'feat'=2] {'region'}, dimensions={0}, use_global_device_ids=true | all-gather | bytes 270336 | tf_op jit(solution)/shard_map/all_gather | solution.py:38
  480.7 16.0 %all-gather.7 = bf16[64,8,512]{2,1,0:T(8,128)(2,1)S(1)} all-gather(bf16[32,8,512]{2,1,0:T(8,128)(2,1)S(1)} %bitcast.195), channel_id=9, replica_groups=mesh['ens'=4,'region'=32,'feat'=2] {'feat'}, dimensions={0}, use_global_device_ids=true | all-gather | bytes 786432 | tf_op jit(solution)/shard_map/all_gather | solution.py:38
  496.9 2.0 collective-permute-start.2
  498.8 2.7 collective-permute-start.3
  501.5 2.2 fusion.19
  503.7 2.1 fusion.22
  505.9 9.2 %gather_fusion.5 = bf16[2048,512]{1,0:T(8,128)(2,1)} fusion(bf16[1024,512]{1,0:T(8,128)(2,1)S(1)} %pad_maximum_fusion.1, s32[2048]{0:T(1024)S(1)} %broadcast_clamp_fusion.1), kind=kCustom, calls=%fused_computation.5 | custom fusion | bytes 4202496 | tf_op jit(solution)/shard_map/gather | solution.py:151
  515.1 7.5 %fusion.63 = (f32[2048]{0:T(1024)S(1)}, f32[2048,512]{1,0:T(8,128)}) fusion(bf16[1,4,512,512]{3,2,1,0:T(8,128)(2,1)} %all-gather.25.cloned.1.call-done, bf16[2048,512]{1,0:T(8,128)(2,1)} %gather_fusion.5, f32[256,512]{1,0:T(8,128)} %fusion.19, bf16[2048,512]{1,0:T(8,128)(2,1)S(1)} %copy-done.5, bf16[256,8,512]{2,1,0:T(8,128)(2,1)} %param.18), kind=kOutput, calls=%fused_computation.145 | convolution fusion | flops 2161113088 | bytes 12066816 | tf_op jit(solution)/shard_map/dot_general | solution.py:61
  522.7 3.0 multiply_reduce_fusion
  525.7 0.4 copy-done.4
  526.1 1.8 fusion.3
  527.9 1.9 fusion.66
  529.8 0.2 multiply_reduce_fusion.3
  530.0 0.9 add_convert_fusion.1
  (84 shorter events, 2.3 us)
Async XLA Ops:
  6.5 78.0 %copy-start = (bf16[1024,512]{1,0:T(8,128)(2,1)S(1)}, bf16[1024,512]{1,0:T(8,128)(2,1)}, u32[]{:S(2)}) copy-start(bf16[1024,512]{1,0:T(8,128)(2,1)} %param.13) | copy-start | bytes 3145732
  6.6 20.0 %copy-start.10 = (s32[1024,1]{0,1:T(1,128)S(1)}, s32[1024,1]{0,1:T(1,128)}, u32[]{:S(2)}) copy-start(s32[1024,1]{0,1:T(1,128)} %param.15) | copy-start | bytes 12292
  6.6 24.5 %copy-start.2 = (s32[1024]{0:T(1024)S(1)}, s32[1024]{0:T(1024)}, u32[]{:S(2)}) copy-start(s32[1024]{0:T(1024)} %param.16) | copy-start | bytes 12292
  6.6 72.6 %all-gather.17.cloned.1.call-start = ((), (), s32[]{:S(2)}) async-start(), calls=%async_computation.3 | async-start | bytes 3145728 | tf_op jit(solution)/shard_map/all_gather | solution.py:75
  31.0 48.0 %copy-start.12 = (s32[1024]{0:T(1024)S(1)}, s32[1024]{0:T(1024)}, u32[]{:S(2)}) copy-start(s32[1024]{0:T(1024)} %param.14) | copy-start | bytes 12292
  31.1 48.1 %copy-start.13 = (bf16[512,512]{1,0:T(8,128)(2,1)S(1)}, bf16[512,512]{1,0:T(8,128)(2,1)}, u32[]{:S(2)}) copy-start(bf16[512,512]{1,0:T(8,128)(2,1)} %param.12) | copy-start | bytes 1572868
  44.7 56.3 %all-to-all-start = ((s32[64,1,32]{2,1,0:T(1,128)}), s32[64,1,32]{2,1,0:T(1,128)S(1)}, u32[]{:S(2)}, u32[]{:S(2)}) async-start(s32[64,1,32]{2,1,0:T(1,128)} %bitcast.7), calls=%async_computation | async-start | bytes 65536 | tf_op jit(solution)/shard_map/all_to_all | solution.py:118
  101.0 18.8 %copy-start.6 = (bf16[2,4,512,256]{3,2,1,0:T(8,128)(2,1)S(1)}, bf16[2,4,512,256]{3,2,1,0:T(8,128)(2,1)}, u32[]{:S(2)}) copy-start(bf16[2,4,512,256]{3,2,1,0:T(8,128)(2,1)} %param.22) | copy-start | bytes 6291460
  101.0 215.4 %all-to-all-start.1 = ((bf16[64,32,512]{2,1,0:T(8,128)(2,1)}), bf16[64,32,512]{2,1,0:T(8,128)(2,1)}, u32[]{:S(2)}, u32[]{:S(2)}) async-start(bf16[64,32,512]{2,1,0:T(8,128)(2,1)} %bitcast.189), calls=%async_computation.1 | async-start | bytes 4194304 | tf_op jit(solution)/shard_map/all_to_all | solution.py:117
  118.9 31.6 %all-gather.15.cloned.1.call-start = ((), (), s32[]{:S(2)}) async-start(), calls=%async_computation.2 | async-start | bytes 2359296 | tf_op jit(solution)/shard_map/all_gather | solution.py:75
  119.7 226.9 %all-gather.21.cloned.1.call-start = ((), (), s32[]{:S(2)}) async-start(), calls=%async_computation.5 | async-start | bytes 3145728 | tf_op jit(solution)/shard_map/all_gather | solution.py:75
  121.4 291.2 %all-gather.19.cloned.1.call-start = ((), (), s32[]{:S(2)}) async-start(), calls=%async_computation.4 | async-start | bytes 2359296 | tf_op jit(solution)/shard_map/all_gather | solution.py:75
  124.0 1.4 copy-start.11
  124.0 26.4 %copy-start.7 = (bf16[256,512]{1,0:T(8,128)(2,1)S(1)}, bf16[256,512]{1,0:T(8,128)(2,1)}, u32[]{:S(2)}) copy-start(bf16[256,512]{1,0:T(8,128)(2,1)} %param.17) | copy-start | bytes 786436
  124.1 316.1 %all-gather.25.cloned.1.call-start = ((), (), s32[]{:S(2)}) async-start(), calls=%async_computation.7 | async-start | bytes 3145728 | tf_op jit(solution)/shard_map/all_gather | solution.py:75
  124.8 378.9 %all-gather.23.cloned.1.call-start = ((), (), s32[]{:S(2)}) async-start(), calls=%async_computation.6 | async-start | bytes 2359296 | tf_op jit(solution)/shard_map/all_gather | solution.py:75
  324.5 19.8 %copy-start.8 = (f32[256,512]{1,0:T(8,128)S(1)}, f32[256,512]{1,0:T(8,128)}, u32[]{:S(2)}) copy-start(f32[256,512]{1,0:T(8,128)} %fusion.27) | copy-start | bytes 1572868
  405.2 8.7 %collective-permute-start = (bf16[128,512]{1,0:T(8,128)(2,1)S(1)}, bf16[128,512]{1,0:T(8,128)(2,1)S(1)}, u32[]{:S(2)}, u32[]{:S(2)}) collective-permute-start(bf16[128,512]{1,0:T(8,128)(2,1)S(1)} %get-tuple-element.13), channel_id=1, source_target_pairs={{0,1},{1,2},{2,3},{3,4},{4,5},{5,6},{6,7},{7,8},{8,9},{9,10},{10,1... | collective-permute-start | bytes 393224 | tf_op jit(solution)/shard_map/ppermute | solution.py:17
  409.0 6.3 %collective-permute-start.1 = (bf16[128,512]{1,0:T(8,128)(2,1)S(1)}, bf16[128,512]{1,0:T(8,128)(2,1)S(1)}, u32[]{:S(2)}, u32[]{:S(2)}) collective-permute-start(bf16[128,512]{1,0:T(8,128)(2,1)S(1)} %get-tuple-element.14), channel_id=1, source_target_pairs={{1,0},{2,1},{3,2},{4,3},{5,4},{6,5},{7,6},{8,7},{9,8},{10,9},{11,1... | collective-permute-start | bytes 393224 | tf_op jit(solution)/shard_map/ppermute | solution.py:18
  431.8 3.4 copy-start.3
  496.9 9.0 %collective-permute-start.2 = (bf16[128,512]{1,0:T(8,128)(2,1)S(1)}, bf16[128,512]{1,0:T(8,128)(2,1)S(1)}, u32[]{:S(2)}, u32[]{:S(2)}) collective-permute-start(bf16[128,512]{1,0:T(8,128)(2,1)S(1)} %get-tuple-element.11), channel_id=1, source_target_pairs={{0,1},{1,2},{2,3},{3,4},{4,5},{5,6},{6,7},{7,8},{8,9},{9,10},{10,1... | collective-permute-start | bytes 393224 | tf_op jit(solution)/shard_map/ppermute | solution.py:17
  498.8 7.0 %collective-permute-start.3 = (bf16[128,512]{1,0:T(8,128)(2,1)S(1)}, bf16[128,512]{1,0:T(8,128)(2,1)S(1)}, u32[]{:S(2)}, u32[]{:S(2)}) collective-permute-start(bf16[128,512]{1,0:T(8,128)(2,1)S(1)} %get-tuple-element.12), channel_id=1, source_target_pairs={{1,0},{2,1},{3,2},{4,3},{5,4},{6,5},{7,6},{8,7},{9,8},{10,9},{11,1... | collective-permute-start | bytes 393224 | tf_op jit(solution)/shard_map/ppermute | solution.py:18
  505.9 9.2 %copy-start.5 = (bf16[2048,512]{1,0:T(8,128)(2,1)S(1)}, bf16[2048,512]{1,0:T(8,128)(2,1)}, u32[]{:S(2)}) copy-start(bf16[2048,512]{1,0:T(8,128)(2,1)} %get-tuple-element.6) | copy-start | bytes 6291460
  522.7 3.4 copy-start.4
  526.1 1.8 copy-start.9
  526.1 4.7 copy-start.1
Sparse Core Ops, SparseCore 0:
  9.2 40.6 all-gather.16
  121.6 28.8 all-gather.14
  152.3 28.3 all-gather.20
  182.4 27.6 all-gather.18
  211.8 28.3 all-gather.24
  241.9 27.6 all-gather.22
where the time goes:
time: 539 us; the launch traced here: 538 us
  waiting for transfers between devices  189 us (35%)
  blocking collectives  112 us (21%)
  local copies, waits for them, and re-layouts  68.2 us (13%)
  starting transfers between devices  63.4 us (12%)
  other arithmetic  52 us (10%)
  matrix products  39 us (7%)
  between operations  14.1 us (3%)
    all_to_all x1, waiting for transfers between devices, on_device(): lax.all_to_all(packed, ('region', 'feat'), split_axis=0, concat_axis=0, t...  155 us
    all_gather x4, blocking collectives, all_blocks(): pieces = lax.all_gather(pieces, axes[k])  112 us
    all_to_all x1, starting transfers between devices, on_device(): lax.all_to_all(row_slots, ('region', 'feat'), split_axis=0, concat_axis=0...  34.3 us
    all_gather x6, waiting for transfers between devices, widen(): return lax.all_gather(stack, 'feat', axis=2, tiled=True)  24.4 us
    gather x2, local copies, waits for them, and re-layouts, on_device(): table[table_index].astype(jnp.float32)  18.4 us
    another operation x2, other arithmetic  18 us
    all_to_all x1, starting transfers between devices, on_device(): lax.all_to_all(packed, ('region', 'feat'), split_axis=0, concat_axis=0, t...  17.9 us
    dot_general x3, matrix products, edge_output(): jnp.dot(hidden, matrix, preferred_element_type=jnp.float32)  17.1 us
  transfers between devices with their start and end apart: 12, of which 4 were waited for; matrix products, arithmetic and copies ran while one was open for 25% of the time, Pallas kernels for 0%

commit v1 on v0

--- a/solution.py
+++ b/solution.py
@@ -72,7 +72,9 @@
 
 
 def widen(stack):
-    return lax.all_gather(stack, "feat", axis=2, tiled=True)
+    return jnp.concatenate(
+        lax.all_to_all(jnp.stack([stack] * lax.axis_size("feat")), "feat", 0, 0), axis=2
+    )
 
 
 def on_device(

time: 539 us -> 608 us (1.13); the launches traced: 538 us -> 598 us
  local copies, waits for them, and re-layouts: 68.2 us -> 111 us
  blocking collectives: 112 us -> 138 us
  between operations: 14.1 us -> 1.08 us
  other arithmetic: 52 us -> 63.3 us
  matrix products: 39 us -> 31.2 us
    all_to_all x0 -> x2, starting transfers between devices: none -> 28.8 us  [widen(): lax.all_to_all(jnp.stack([stack] * lax.axis_size('feat')), 'feat', 0, 0)]
    all_to_all x0 -> x4, blocking collectives: none -> 24.7 us  [widen(): lax.all_to_all(jnp.stack([stack] * lax.axis_size('feat')), 'feat', 0, 0)]
    all_gather x6 -> x0, waiting for transfers between devices: 24.4 us -> none  [widen(): return lax.all_gather(stack, 'feat', axis=2, tiled=True)]
    all_to_all x1, waiting for transfers between devices: 155 us -> 176 us  [on_device(): lax.all_to_all(packed, ('region', 'feat'), split_axis=0, concat_axis=0, t...]
    all_to_all x1, starting transfers between devices: 34.3 us -> 14.3 us  [on_device(): lax.all_to_all(row_slots, ('region', 'feat'), split_axis=0, concat_axis=0...]
    convert_element_type x0 -> x7, local copies, waits for them, and re-layouts: none -> 17.8 us  [the longest x4 16 us: on_device(): jnp.repeat(receiver, kdeg, axis=0).astype(jnp.float32)]
    unnamed x29 -> x85, local copies, waits for them, and re-layouts: 0.94 us -> 12.8 us
    another operation x2 -> x8, other arithmetic: 18 us -> 29.3 us
  transfers between devices with their start and end apart: 12 -> 8, of which waited for: 4 -> 2; matrix products, arithmetic and copies ran while one was open for 25% -> 19% of each run, Pallas kernels for 0% -> 0%
where the time goes in v1:
time: 608 us; the launch traced here: 598 us
  waiting for transfers between devices  184 us (30%)
  blocking collectives  138 us (23%)
  local copies, waits for them, and re-layouts  111 us (18%)
  starting transfers between devices  68.9 us (11%)
  other arithmetic  63.3 us (10%)
  matrix products  31.2 us (5%)
    all_to_all x1, waiting for transfers between devices, on_device(): lax.all_to_all(packed, ('region', 'feat'), split_axis=0, concat_axis=0, t...  176 us
    all_gather x4, blocking collectives, all_blocks(): pieces = lax.all_gather(pieces, axes[k])  114 us
    all_to_all x2, starting transfers between devices, widen(): lax.all_to_all(jnp.stack([stack] * lax.axis_size('feat')), 'feat', 0, 0)  28.8 us
    all_to_all x4, blocking collectives, widen(): lax.all_to_all(jnp.stack([stack] * lax.axis_size('feat')), 'feat', 0, 0)  24.7 us
    gather x4, local copies, waits for them, and re-layouts, on_device(): table[table_index].astype(jnp.float32)  20.1 us
    dot_general x3, matrix products, edge_output(): jnp.dot(hidden, matrix, preferred_element_type=jnp.float32)  18.5 us
    another operation x2, other arithmetic  18 us
    convert_element_type x4, local copies, waits for them, and re-layouts, on_device(): jnp.repeat(receiver, kdeg, axis=0).astype(jnp.float32)  16 us
  transfers between devices with their start and end apart: 8, of which 2 were waited for; matrix products, arithmetic and copies ran while one was open for 19% of the time, Pallas kernels for 0%

profile of v1, /device:TPU:37, one launch (start us, length us, event | category | flops | bytes accessed | tf_op | source)
XLA Modules:
  0.0 597.9 jit_solution(13937337593221986939)
XLA Ops:
  0.0 1.6 copy.60
  1.6 1.5 pad_maximum_fusion
  3.1 24.2 %all-to-all-start.2 = ((bf16[2,4,512,256]{2,3,1,0:T(8,128)(2,1)}), bf16[2,4,512,256]{2,3,1,0:T(8,128)(2,1)S(1)}, u32[]{:S(2)}, u32[]{:S(2)}) async-start(bf16[2,4,512,256]{2,3,1,0:T(8,128)(2,1)} %pad_maximum_fusion), calls=%async_computation.2 | async-start | bytes 4194304 | tf_op jit(solution)/shard_map/all_to_all | solution.py:76
  27.3 2.3 copy.55
  29.6 2.7 pad_maximum_fusion.3
  32.3 4.6 all-to-all-start
  39.2 4.0 gather_fusion.1
  43.2 1.3 copy.63
  44.5 18.0 %reduce-window.6 = s32[64,8,128]{2,1,0:T(8,128)S(1)} reduce-window(s32[64,8,128]{2,1,0:T(8,128)S(1)} %fusion.40, s32[]{:T(128)} %constant.81.clone.1), window={size=1x1x128 pad=0_0x0_0x127_0}, to_apply=%region_0.0 | reduce-window | flops 8323072 | bytes 524292 | tf_op jit(solution)/shard_map/reduce-window
  63.1 4.3 scatter_custom_fusion.1
  67.5 8.6 %gather_fusion = s32[2048]{0:T(1024)S(1)} fusion(s32[1024]{0:T(1024)S(1)} %copy-done.2, s32[2048]{0:T(1024)S(1)} %fusion.41), kind=kCustom, calls=%fused_computation | custom fusion | bytes 24576 | tf_op jit(solution)/shard_map/gather | solution.py:114
  76.1 4.3 scatter_custom_fusion
  81.2 2.8 fusion.53
  83.9 1.5 copy.95
  85.4 1.5 pad_maximum_fusion.1
  89.6 2.8 pad_maximum_fusion.4
  93.0 1.5 pad_maximum_fusion.2
  94.7 1.3 pad_maximum_fusion.5
  96.0 6.4 %all_to_all.44 = bf16[2,4,512,256]{2,3,1,0:T(8,128)(2,1)S(1)} all-to-all(bf16[2,4,512,256]{2,3,1,0:T(8,128)(2,1)} %pad_maximum_fusion.1), channel_id=1, replica_groups=mesh['ens'=4,'region'=32,'feat'=2] {'feat'}, dimensions={0} | all-to-all | bytes 4194304 | tf_op jit(solution)/shard_map/all_to_all | solution.py:76
  102.5 6.0 %all_to_all.45 = bf16[2,3,512,256]{2,3,1,0:T(8,128)(2,1)} all-to-all(bf16[2,3,512,256]{2,3,1,0:T(8,128)(2,1)S(1)} %copy-done.11), channel_id=1, replica_groups=mesh['ens'=4,'region'=32,'feat'=2] {'feat'}, dimensions={0} | all-to-all | bytes 3145728 | tf_op jit(solution)/shard_map/all_to_all | solution.py:76
  108.5 6.4 %all_to_all.46 = bf16[2,4,512,256]{2,3,1,0:T(8,128)(2,1)} all-to-all(bf16[2,4,512,256]{2,3,1,0:T(8,128)(2,1)S(1)} %copy-done.6), channel_id=1, replica_groups=mesh['ens'=4,'region'=32,'feat'=2] {'feat'}, dimensions={0} | all-to-all | bytes 4194304 | tf_op jit(solution)/shard_map/all_to_all | solution.py:76
  115.0 5.8 all_to_all.47
  120.8 14.3 %all-to-all-start.1 = ((s32[64,1,32]{2,1,0:T(1,128)}), s32[64,1,32]{2,1,0:T(1,128)S(1)}, u32[]{:S(2)}, u32[]{:S(2)}) async-start(s32[64,1,32]{2,1,0:T(1,128)} %bitcast.10), calls=%async_computation.1 | async-start | bytes 65536 | tf_op jit(solution)/shard_map/all_to_all | solution.py:120
  135.1 3.1 fusion.10
  138.2 1.5 copy.64
  139.7 9.2 %gather_fusion.2 = bf16[2048,512]{1,0:T(8,128)(2,1)} fusion(bf16[1024,512]{1,0:T(8,128)(2,1)S(1)} %copy.64, s32[2048]{0:T(1024)S(1)} %fusion.41), kind=kCustom, calls=%fused_computation.2 | custom fusion | bytes 4202496 | tf_op jit(solution)/shard_map/gather | solution.py:117
  148.9 8.2 %all-to-all-done.1 = s32[64,1,32]{2,1,0:T(1,128)S(1)} async-done(((s32[64,1,32]{2,1,0:T(1,128)}), s32[64,1,32]{2,1,0:T(1,128)S(1)}, u32[]{:S(2)}, u32[]{:S(2)}) %all-to-all-start.1) | async-done | bytes 8224 | tf_op jit(solution)/shard_map/all_to_all | solution.py:120
  157.1 15.3 %all-to-all-start.3 = ((bf16[64,32,512]{2,1,0:T(8,128)(2,1)}), bf16[64,32,512]{2,1,0:T(8,128)(2,1)}, u32[]{:S(2)}, u32[]{:S(2)}) async-start(bf16[64,32,512]{2,1,0:T(8,128)(2,1)} %bitcast.17), calls=%async_computation.3 | async-start | bytes 4194304 | tf_op jit(solution)/shard_map/all_to_all | solution.py:119
  173.1 1.6 copy.111
  176.3 1.4 copy-done.5
  177.8 1.3 copy-done.10
  182.9 1.4 fusion.54
  184.3 1.4 fusion.52
  186.1 7.5 %gather_fusion.3 = bf16[2048,512]{1,0:T(8,128)(2,1)S(1)} fusion(bf16[256,512]{1,0:T(8,128)(2,1)S(1)} %copy.65, s32[2048]{0:T(1024)S(1)} %broadcast_clamp_fusion), kind=kCustom, calls=%fused_computation.3 | custom fusion | bytes 4202496 | tf_op jit(solution)/shard_map/gather | solution.py:124
  193.6 176.2 %all-to-all-done.3 = bf16[64,32,512]{2,1,0:T(8,128)(2,1)} async-done(((bf16[64,32,512]{2,1,0:T(8,128)(2,1)}), bf16[64,32,512]{2,1,0:T(8,128)(2,1)}, u32[]{:S(2)}, u32[]{:S(2)}) %all-to-all-start.3) | async-done | bytes 2097184 | tf_op jit(solution)/shard_map/all_to_all | solution.py:119
  369.8 2.8 multiply_convert_fusion.5
  372.6 1.3 fusion.62
  374.5 2.5 convert_select_fusion
  377.0 5.4 copy.66
  382.3 14.4 %scatter_custom_fusion.2 = f32[256,512]{1,0:T(8,128)S(1)} fusion(s32[2048]{0:T(1024)S(1)} %reshape.420, f32[2048,512]{1,0:T(8,128)} %copy.66, f32[]{:T(128)} %constant.78.clone.1), kind=kCustom, calls=%fused_computation.90 | custom fusion | flops 1048576 | bytes 524800 | tf_op jit(solution)/shard_map/scatter-add | solution.py:129
  397.1 2.0 fusion.63
  399.9 38.9 %all-gather = bf16[256,512]{1,0:T(8,128)(2,1)S(1)} all-gather(bf16[8,512]{1,0:T(8,128)(2,1)S(1)} %slice.179), channel_id=2, replica_groups=mesh['ens'=4,'region'=32,'feat'=2] {'region'}, dimensions={0}, use_global_device_ids=true | all-gather | bytes 270336 | tf_op jit(solution)/shard_map/all_gather | solution.py:38
  438.8 18.3 %all-gather.1 = bf16[64,8,512]{2,1,0:T(8,128)(2,1)S(1)} all-gather(bf16[32,8,512]{2,1,0:T(8,128)(2,1)S(1)} %bitcast.191), channel_id=3, replica_groups=mesh['ens'=4,'region'=32,'feat'=2] {'feat'}, dimensions={0}, use_global_device_ids=true | all-gather | bytes 786432 | tf_op jit(solution)/shard_map/all_gather | solution.py:38
  457.2 3.8 collective-permute-start
  461.0 2.1 collective-permute-start.1
  463.4 2.5 broadcast_bitcast_fusion.1
  466.0 5.5 copy.75
  472.7 7.5 %gather_fusion.4 = bf16[2048,512]{1,0:T(8,128)(2,1)S(1)} fusion(bf16[1024,512]{1,0:T(8,128)(2,1)S(1)} %pad_maximum_fusion.6, s32[2048]{0:T(1024)S(1)} %broadcast_clamp_fusion.1), kind=kCustom, calls=%fused_computation.4 | custom fusion | bytes 4202496 | tf_op jit(solution)/shard_map/gather | solution.py:153
  480.2 2.5 copy.74
  482.7 8.2 %fusion.64 = (f32[2048]{0:T(1024)S(1)}, f32[2048,512]{1,0:T(8,128)}) fusion(bf16[512,512]{0,1:T(8,128)(2,1)S(1)} %bitcast.203, f32[2048,512]{0,1:T(8,128)} %copy.75, bf16[2048,512]{0,1:T(8,128)(2,1)} %copy.74, bf16[512,512]{0,1:T(8,128)(2,1)S(1)} %bitcast.202, bf16[256,8,512]{2,1,0:T(8,128)(2,1)} %param.18), kind=kOutput, calls=%fused_computation.143 | convolution fusion | flops 2156918784 | bytes 13639680 | tf_op jit(solution)/shard_map/dot_general | solution.py:61
  491.0 3.0 multiply_reduce_fusion.1
  494.4 2.6 fusion
  498.8 39.1 %all-gather.2 = bf16[256,512]{1,0:T(8,128)(2,1)S(1)} all-gather(bf16[8,512]{1,0:T(8,128)(2,1)S(1)} %slice.189), channel_id=4, replica_groups=mesh['ens'=4,'region'=32,'feat'=2] {'region'}, dimensions={0}, use_global_device_ids=true | all-gather | bytes 270336 | tf_op jit(solution)/shard_map/all_gather | solution.py:38
  537.9 17.4 %all-gather.3 = bf16[64,8,512]{2,1,0:T(8,128)(2,1)S(1)} all-gather(bf16[32,8,512]{2,1,0:T(8,128)(2,1)S(1)} %bitcast.192), channel_id=5, replica_groups=mesh['ens'=4,'region'=32,'feat'=2] {'feat'}, dimensions={0}, use_global_device_ids=true | all-gather | bytes 786432 | tf_op jit(solution)/shard_map/all_gather | solution.py:38
  555.4 2.0 collective-permute-start.2
  557.4 2.7 collective-permute-start.3
  560.4 2.5 broadcast_bitcast_fusion
  562.9 5.5 copy.85
  569.6 7.5 %gather_fusion.5 = bf16[2048,512]{1,0:T(8,128)(2,1)S(1)} fusion(bf16[1024,512]{1,0:T(8,128)(2,1)S(1)} %pad_maximum_fusion.7, s32[2048]{0:T(1024)S(1)} %broadcast_clamp_fusion.1), kind=kCustom, calls=%fused_computation.5 | custom fusion | bytes 4202496 | tf_op jit(solution)/shard_map/gather | solution.py:153
  577.2 2.5 copy.83
  579.6 9.0 %fusion.68 = (f32[2048]{0:T(1024)S(1)}, f32[2048,512]{1,0:T(8,128)}) fusion(bf16[512,512]{0,1:T(8,128)(2,1)S(1)} %bitcast.201, f32[2048,512]{0,1:T(8,128)} %copy.85, bf16[2048,512]{0,1:T(8,128)(2,1)} %copy.83, bf16[512,512]{0,1:T(8,128)(2,1)S(1)} %bitcast.200, bf16[2048,512]{1,0:T(8,128)(2,1)} %get-tuple-element.6, bf16[256,8,512]{2,1,0:T(8,128)(2,1)} %param.18), kind=kOutput, calls=%fused_computation.145 | convolution fusion | flops 2161113088 | bytes 15736832 | tf_op jit(solution)/shard_map/dot_general | solution.py:61
  588.7 3.0 multiply_reduce_fusion
  592.1 2.5 fusion.4
  594.6 1.9 fusion.71
  (158 shorter events, 22.0 us)
Async XLA Ops:
  0.0 135.1 %copy-start = (bf16[1024,512]{1,0:T(8,128)(2,1)S(1)}, bf16[1024,512]{1,0:T(8,128)(2,1)}, u32[]{:S(2)}) copy-start(bf16[1024,512]{1,0:T(8,128)(2,1)} %param.13) | copy-start | bytes 3145732
  3.1 29.2 %all-to-all-start.2 = ((bf16[2,4,512,256]{2,3,1,0:T(8,128)(2,1)}), bf16[2,4,512,256]{2,3,1,0:T(8,128)(2,1)S(1)}, u32[]{:S(2)}, u32[]{:S(2)}) async-start(bf16[2,4,512,256]{2,3,1,0:T(8,128)(2,1)} %pad_maximum_fusion), calls=%async_computation.2 | async-start | bytes 4194304 | tf_op jit(solution)/shard_map/all_to_all | solution.py:76
  32.3 63.7 %all-to-all-start = ((bf16[2,3,512,256]{2,3,1,0:T(8,128)(2,1)}), bf16[2,3,512,256]{2,3,1,0:T(8,128)(2,1)}, u32[]{:S(2)}, u32[]{:S(2)}) async-start(bf16[2,3,512,256]{2,3,1,0:T(8,128)(2,1)} %pad_maximum_fusion.3), calls=%async_computation | async-start | bytes 3145728 | tf_op jit(solution)/shard_map/all_to_all | solution.py:76
  37.2 1.3 copy-start.24
  38.4 0.7 copy-start.38
  43.1 1.3 copy-start.36
  43.1 24.3 %copy-start.2 = (s32[1024]{0:T(1024)S(1)}, s32[1024]{0:T(1024)}, u32[]{:S(2)}) copy-start(s32[1024]{0:T(1024)} %param.16) | copy-start | bytes 12292
  85.4 2.1 copy-start.22
  92.9 1.5 copy-start.13
  96.0 6.4 %copy-start.11 = (bf16[2,3,512,256]{2,3,1,0:T(8,128)(2,1)S(1)}, bf16[2,3,512,256]{2,3,1,0:T(8,128)(2,1)}, u32[]{:S(2)}) copy-start(bf16[2,3,512,256]{2,3,1,0:T(8,128)(2,1)} %pad_maximum_fusion.4) | copy-start | bytes 4718596
  102.5 6.0 %copy-start.6 = (bf16[2,4,512,256]{2,3,1,0:T(8,128)(2,1)S(1)}, bf16[2,4,512,256]{2,3,1,0:T(8,128)(2,1)}, u32[]{:S(2)}) copy-start(bf16[2,4,512,256]{2,3,1,0:T(8,128)(2,1)} %pad_maximum_fusion.2) | copy-start | bytes 6291460
  108.5 6.4 %copy-start.12 = (bf16[2,3,512,256]{2,3,1,0:T(8,128)(2,1)S(1)}, bf16[2,3,512,256]{2,3,1,0:T(8,128)(2,1)}, u32[]{:S(2)}) copy-start(bf16[2,3,512,256]{2,3,1,0:T(8,128)(2,1)} %pad_maximum_fusion.5) | copy-start | bytes 4718596
  120.8 36.3 %all-to-all-start.1 = ((s32[64,1,32]{2,1,0:T(1,128)}), s32[64,1,32]{2,1,0:T(1,128)S(1)}, u32[]{:S(2)}, u32[]{:S(2)}) async-start(s32[64,1,32]{2,1,0:T(1,128)} %bitcast.10), calls=%async_computation.1 | async-start | bytes 65536 | tf_op jit(solution)/shard_map/all_to_all | solution.py:120
  157.0 15.3 %copy-start.19 = (bf16[1,512,2,256]{1,3,2,0:T(8,128)(2,1)S(1)}, bf16[1,512,2,256]{1,3,2,0:T(8,128)(2,1)}, u32[]{:S(2)}) copy-start(bf16[1,512,2,256]{1,3,2,0:T(8,128)(2,1)} %get-tuple-element.18) | copy-start | bytes 1572868
  157.1 15.3 %copy-start.23 = (bf16[256,512]{1,0:T(8,128)(2,1)S(1)}, bf16[256,512]{1,0:T(8,128)(2,1)}, u32[]{:S(2)}) copy-start(bf16[256,512]{1,0:T(8,128)(2,1)} %param.17) | copy-start | bytes 786436
  157.1 15.8 %copy-start.37 = (s32[256,8]{0,1:T(8,128)S(1)}, s32[256,8]{0,1:T(8,128)}, u32[]{:S(2)}) copy-start(s32[256,8]{0,1:T(8,128)} %param.19) | copy-start | bytes 24580
  157.1 212.7 %all-to-all-start.3 = ((bf16[64,32,512]{2,1,0:T(8,128)(2,1)}), bf16[64,32,512]{2,1,0:T(8,128)(2,1)}, u32[]{:S(2)}, u32[]{:S(2)}) async-start(bf16[64,32,512]{2,1,0:T(8,128)(2,1)} %bitcast.17), calls=%async_computation.3 | async-start | bytes 4194304 | tf_op jit(solution)/shard_map/all_to_all | solution.py:119
  174.7 1.4 copy-start.9
  176.1 1.6 copy-start.5
  177.7 1.4 copy-start.10
  369.8 2.8 copy-start.16
  382.3 14.8 %copy-start.31 = (bf16[1,512,2,256]{1,3,2,0:T(8,128)(2,1)S(1)}, bf16[1,512,2,256]{1,3,2,0:T(8,128)(2,1)}, u32[]{:S(2)}) copy-start(bf16[1,512,2,256]{1,3,2,0:T(8,128)(2,1)} %get-tuple-element.29) | copy-start | bytes 1572868
  397.1 2.4 copy-start.21
  399.5 71.9 %copy-start.7 = (bf16[256,512]{1,0:T(8,128)(2,1)}, bf16[256,512]{1,0:T(8,128)(2,1)S(1)}, u32[]{:S(2)}) copy-start(bf16[256,512]{1,0:T(8,128)(2,1)S(1)} %add_convert_fusion.2) | copy-start | bytes 786436
  399.5 63.6 %copy-start.20 = (bf16[1,512,2,256]{1,3,2,0:T(8,128)(2,1)S(1)}, bf16[1,512,2,256]{1,3,2,0:T(8,128)(2,1)}, u32[]{:S(2)}) copy-start(bf16[1,512,2,256]{1,3,2,0:T(8,128)(2,1)} %get-tuple-element.15) | copy-start | bytes 1572868
  457.2 15.4 %collective-permute-start = (bf16[128,512]{1,0:T(8,128)(2,1)S(1)}, bf16[128,512]{1,0:T(8,128)(2,1)S(1)}, u32[]{:S(2)}, u32[]{:S(2)}) collective-permute-start(bf16[128,512]{1,0:T(8,128)(2,1)S(1)} %get-tuple-element.34), channel_id=1, source_target_pairs={{0,1},{1,2},{2,3},{3,4},{4,5},{5,6},{6,7},{7,8},{8,9},{9,10},{10,1... | collective-permute-start | bytes 393224 | tf_op jit(solution)/shard_map/ppermute | solution.py:17
  461.0 11.6 %collective-permute-start.1 = (bf16[128,512]{1,0:T(8,128)(2,1)S(1)}, bf16[128,512]{1,0:T(8,128)(2,1)S(1)}, u32[]{:S(2)}, u32[]{:S(2)}) collective-permute-start(bf16[128,512]{1,0:T(8,128)(2,1)S(1)} %get-tuple-element.35), channel_id=1, source_target_pairs={{1,0},{2,1},{3,2},{4,3},{5,4},{6,5},{7,6},{8,7},{9,8},{10,9},{11,1... | collective-permute-start | bytes 393224 | tf_op jit(solution)/shard_map/ppermute | solution.py:18
  466.0 5.5 copy-start.15
  480.2 2.5 copy-start.34
  480.2 2.5 copy-start.35
  491.0 3.4 copy-start.3
  494.4 2.6 copy-start.26
  494.4 2.6 copy-start.29
  494.4 2.7 copy-start.30
  497.1 1.2 copy-start.8
  497.1 1.3 copy-start.18
  498.4 61.6 %copy-start.17 = (bf16[1,512,2,256]{1,3,2,0:T(8,128)(2,1)S(1)}, bf16[1,512,2,256]{1,3,2,0:T(8,128)(2,1)}, u32[]{:S(2)}) copy-start(bf16[1,512,2,256]{1,3,2,0:T(8,128)(2,1)} %get-tuple-element.9) | copy-start | bytes 1572868
  555.4 14.1 %collective-permute-start.2 = (bf16[128,512]{1,0:T(8,128)(2,1)S(1)}, bf16[128,512]{1,0:T(8,128)(2,1)S(1)}, u32[]{:S(2)}, u32[]{:S(2)}) collective-permute-start(bf16[128,512]{1,0:T(8,128)(2,1)S(1)} %get-tuple-element.32), channel_id=1, source_target_pairs={{0,1},{1,2},{2,3},{3,4},{4,5},{5,6},{6,7},{7,8},{8,9},{9,10},{10,1... | collective-permute-start | bytes 393224 | tf_op jit(solution)/shard_map/ppermute | solution.py:17
  557.4 12.2 %collective-permute-start.3 = (bf16[128,512]{1,0:T(8,128)(2,1)S(1)}, bf16[128,512]{1,0:T(8,128)(2,1)S(1)}, u32[]{:S(2)}, u32[]{:S(2)}) collective-permute-start(bf16[128,512]{1,0:T(8,128)(2,1)S(1)} %get-tuple-element.33), channel_id=1, source_target_pairs={{1,0},{2,1},{3,2},{4,3},{5,4},{6,5},{7,6},{8,7},{9,8},{10,9},{11,1... | collective-permute-start | bytes 393224 | tf_op jit(solution)/shard_map/ppermute | solution.py:18
  562.9 5.5 copy-start.14
  577.1 2.5 copy-start.32
  577.2 2.5 copy-start.33
  588.7 3.4 copy-start.4
  592.1 2.5 copy-start.25
  592.1 2.5 copy-start.27
  592.1 2.5 copy-start.28
  594.6 3.1 copy-start.1
